TPU v7x, 32 devices: a whole 2x2x4 slice. The times are simulated.
32 devices in a mesh: img: 8 (over y, x, core), cls: 4 (over z).
Axes of the slice: x: 2, y: 2, z: 4, core: 2. Of those that a mesh axis runs over, the one named last changes fastest.
Arguments:
- images: bfloat16 [64, 9216], P('img'), may hold values from -64 to 64
- references: bfloat16 [512, 9216], P(('img', 'cls')), may hold values from -0.2 to 0.2
- class_logprior: bfloat16 [512], P(('img', 'cls')), may hold values from -3 to 3
- ctf_table: float32 [16, 32], replicated, may hold values from -1 to 1, as said below
- noise_power: float32 [32], replicated, may hold values from 0.5 to 2
- tau_power: float32 [32], replicated, may hold values from 0.5 to 4
- defocus: int32 [64], P('img'), may hold values from 0 to 15
- offsets: int32 [64, 4, 2], P('img'), may hold values from -3 to 3
Outputs:
- new_refs: float32 [512, 9216], P(('img', 'cls'))
- new_weights: float32 [512], P(('img', 'cls'))
- loglik: float32 [64], P('img')
Inputs may be any that keep to these rules, and one draw needn't show every extreme that they name: `ctf_table`: each row is a contrast transfer curve that oscillates over the cycles.
All inputs are finite; a program needn't handle non-finite values.
Results may differ from a plain program's by a relative error of at most 0.0068.
Values may be sent and summed in bfloat16 or wider, within the bound.
A program may use at most 64 MiB of HBM per device.

v0:
```python
import math

import jax
import jax.numpy as jnp
import numpy as np
from jax import lax
from jax.experimental import pallas as pl
from jax.experimental.pallas import tpu as pltpu
from jax.sharding import PartitionSpec as P

TRANS = 4
CYCLES = 32
ANG = 144
ROT = 36
NDEF = 16

STRIDE = ANG // ROT
HALF = STRIDE * CYCLES
LANES = 2 * HALF
REACH = 3
SIDE = 2 * REACH + 1
COMBOS = SIDE * SIDE
TABLE_ROWS = 112
BATCH = 4
HIGH = lax.Precision.HIGHEST
offset_sigma = 2.0


def phase_rows():
    turn = np.arange(ROT)[:, None, None]
    step = np.arange(STRIDE)[None, :, None]
    radius = np.arange(CYCLES)[None, None, :] + 1.0
    theta = 2.0 * math.pi * (STRIDE * turn + step) / ANG
    freq_x = (radius * np.cos(theta)).reshape(ROT, 1, HALF)
    freq_y = (radius * np.sin(theta)).reshape(ROT, 1, HALF)
    combo = np.arange(COMBOS)[None, :, None]
    dx = combo // SIDE - REACH
    dy = combo % SIDE - REACH
    angle = -2.0 * math.pi * (dx * freq_x + dy * freq_y) / (2.0 * CYCLES)
    full = np.concatenate([np.cos(angle), np.sin(angle)], axis=2)
    high = full.astype(jnp.bfloat16)
    low = (full - high.astype(np.float64)).astype(jnp.bfloat16)
    table = np.zeros((ROT, TABLE_ROWS, LANES), jnp.bfloat16)
    table[:, :COMBOS] = high
    table[:, COMBOS : 2 * COMBOS] = low
    return table


def turn_major(source):
    shaped = source.reshape(source.shape[0], 2, CYCLES, ROT, STRIDE)
    return shaped.transpose(3, 0, 1, 4, 2).reshape(ROT, source.shape[0], LANES)


def gather_kernel(n, own_ref, all_ref, send_sem, recv_sem, relay_send, relay_recv):
    me = lax.axis_index("img")
    partner = me + 1 - 2 * lax.rem(me, 2)
    peers = [lax.rem(me + 2 * hop, n) for hop in range(1, n // 2)]
    barrier = pltpu.get_barrier_semaphore()
    for peer in [partner] + peers:
        pl.semaphore_signal(
            barrier, inc=1, device_id={"img": peer}, device_id_type=pl.DeviceIdType.MESH
        )
    pl.semaphore_wait(barrier, n // 2)

    def send(src, dst, peer, left, landed):
        copy = pltpu.make_async_remote_copy(
            src_ref=src,
            dst_ref=dst,
            send_sem=left,
            recv_sem=landed,
            device_id={"img": peer},
            device_id_type=pl.DeviceIdType.MESH,
        )
        copy.start()
        return copy

    direct = [
        send(own_ref, all_ref.at[me], peer, send_sem.at[hop], recv_sem.at[hop])
        for hop, peer in enumerate(peers)
    ]
    relays = [send(own_ref, all_ref.at[me], partner, relay_send.at[0], relay_recv.at[0])]
    all_ref[me] = own_ref[...]
    for hop, copy in enumerate(direct):
        copy.wait_recv()
        source = lax.rem(me + n - 2 * (hop + 1), n)
        slot = all_ref.at[source]
        relays.append(
            send(slot, slot, partner, relay_send.at[hop + 1], relay_recv.at[hop + 1])
        )
    for copy in relays:
        copy.wait_recv()
    for copy in direct + relays:
        copy.wait_send()


def gather_images(own, n):
    return pl.pallas_call(
        lambda *refs: gather_kernel(n, *refs),
        out_shape=jax.ShapeDtypeStruct((n,) + own.shape, own.dtype),
        in_specs=[pl.BlockSpec(memory_space=pltpu.VMEM)],
        out_specs=pl.BlockSpec(memory_space=pltpu.VMEM),
        scratch_shapes=[
            pltpu.SemaphoreType.DMA((n // 2,)),
            pltpu.SemaphoreType.DMA((n // 2,)),
            pltpu.SemaphoreType.DMA((n // 2,)),
            pltpu.SemaphoreType.DMA((n // 2,)),
        ],
        compiler_params=pltpu.CompilerParams(collective_id=0, has_side_effects=True),
        name="gather_images",
    )(own)


def exchange_kernel(n, m, own_ref, all_ref, local_sem, cls_send, cls_recv, img_send, img_recv):
    row, column = lax.axis_index("img"), lax.axis_index("cls")
    above = [{"cls": lax.rem(column + hop, m)} for hop in range(1, m)]
    beside = [{"img": lax.rem(row + hop, n)} for hop in range(1, n)]
    barrier = pltpu.get_barrier_semaphore()
    for peer in above + beside:
        pl.semaphore_signal(barrier, inc=1, device_id=peer, device_id_type=pl.DeviceIdType.MESH)
    pl.semaphore_wait(barrier, n + m - 2)

    def send_all(src, dst, peers, left, landed):
        copies = []
        for hop, peer in enumerate(peers):
            copy = pltpu.make_async_remote_copy(
                src_ref=src,
                dst_ref=dst,
                send_sem=left.at[hop],
                recv_sem=landed.at[hop],
                device_id=peer,
                device_id_type=pl.DeviceIdType.MESH,
            )
            copy.start()
            copies.append(copy)
        return copies

    slot = all_ref.at[row, column]
    first = send_all(own_ref, slot, above, cls_send, cls_recv)
    keep = pltpu.make_async_copy(own_ref, slot, local_sem)
    keep.start()
    keep.wait()
    for copy in first:
        copy.wait_recv()
    second = send_all(all_ref.at[row], all_ref.at[row], beside, img_send, img_recv)
    for copy in second:
        copy.wait_recv()
    for copy in first + second:
        copy.wait_send()


def exchange_stats(own, n, m):
    vmem = pl.BlockSpec(memory_space=pltpu.VMEM)
    return pl.pallas_call(
        lambda *refs: exchange_kernel(n, m, *refs),
        out_shape=jax.ShapeDtypeStruct((n, m) + own.shape, own.dtype),
        in_specs=[vmem],
        out_specs=vmem,
        scratch_shapes=[
            pltpu.SemaphoreType.DMA,
            pltpu.SemaphoreType.DMA((m,)),
            pltpu.SemaphoreType.DMA((m,)),
            pltpu.SemaphoreType.DMA((n,)),
            pltpu.SemaphoreType.DMA((n,)),
        ],
        compiler_params=pltpu.CompilerParams(collective_id=1, has_side_effects=True),
        name="exchange_stats",
    )(own)


def score_kernel(
    images_ref, refs_ref, prior_ref, ctf_ref, noise_ref, table_ref,
    ins_ref, expo_ref, stat_ref, square_ref, turned,
):
    n, _, local, _ = images_ref.shape
    owned = refs_ref.shape[1]
    count = n * local
    rows = count * TRANS
    height = ROT * owned
    for spot in range(2 * ROT):
        turned[spot * owned : (spot + 1) * owned] = refs_ref[-spot % ROT]
    meta = images_ref[:, ROT].astype(jnp.float32).reshape(count, LANES)
    group = lax.broadcasted_iota(jnp.int32, (count, NDEF), 1).astype(jnp.float32)
    chosen = (group == meta[:, :1]).astype(jnp.float32)
    contrast = jnp.dot(chosen, ctf_ref[...], precision=HIGH, preferred_element_type=jnp.float32)
    contrast = jnp.concatenate([contrast] * TRANS, axis=0)
    scaled = contrast / noise_ref[...]
    square = contrast * contrast
    square_ref[...] = square
    spot = lax.broadcasted_iota(jnp.int32, (count, TABLE_ROWS), 1).astype(jnp.float32)
    lane = lax.broadcasted_iota(jnp.int32, (count, HALF), 1)
    picks, offset_terms = [], []
    for t in range(TRANS):
        dx = meta[:, 1 + t : 2 + t]
        dy = meta[:, 1 + TRANS + t : 2 + TRANS + t]
        index = (dx + REACH) * SIDE + (dy + REACH)
        hit = (spot == index) | (spot == index + COMBOS)
        picks.append(hit.astype(jnp.float32).astype(jnp.bfloat16))
        value = -(dx * dx + dy * dy) / (2.0 * offset_sigma * offset_sigma)
        offset_terms.append(jnp.where(lane == 0, value, 0.0))
    pick = jnp.concatenate(picks, axis=0)
    offset_term = jnp.concatenate(offset_terms, axis=0)

    power = jnp.zeros((owned, HALF), jnp.float32)
    for b in range(ROT):
        entry = refs_ref[b].astype(jnp.float32)
        squares = entry * entry
        power = power + squares[:, :HALF] + squares[:, HALF:]
    by_lane = (((1,), (1,)), ((), ()))
    norm_coef = square / (2.0 * noise_ref[...])
    base = prior_ref[:, :1] - lax.dot_general(
        power, norm_coef, by_lane, precision=HIGH, preferred_element_type=jnp.float32
    )
    base = base + lax.dot_general(
        jnp.ones((owned, HALF), jnp.float32), offset_term, by_lane,
        precision=HIGH, preferred_element_type=jnp.float32,
    )

    for r in range(ROT):
        expo_ref[r * owned : (r + 1) * owned] = base

    @pl.loop(0, ROT // BATCH)
    def _(batch):
        left, right = [], []
        for part in range(BATCH):
            b = batch * BATCH + part
            phase = jnp.dot(pick, table_ref[b], preferred_element_type=jnp.float32)
            cosine, sine = phase[:, :HALF], phase[:, HALF:]
            picture = images_ref[:, b].astype(jnp.float32).reshape(count, LANES)
            picture = jnp.concatenate([picture] * TRANS, axis=0)
            real, imag = picture[:, :HALF], picture[:, HALF:]
            moved_real = real * cosine - imag * sine
            moved_imag = real * sine + imag * cosine
            ins_ref[b] = jnp.concatenate(
                [moved_real * contrast, moved_imag * contrast], axis=1
            ).astype(jnp.bfloat16)
            right.append(
                jnp.concatenate([moved_real * scaled, moved_imag * scaled], axis=1).astype(
                    jnp.bfloat16
                )
            )
            start = pl.multiple_of((ROT - b) * owned, owned)
            left.append(turned[pl.ds(start, height), :])
        expo_ref[...] += lax.dot_general(
            jnp.concatenate(left, axis=1), jnp.concatenate(right, axis=1), by_lane,
            preferred_element_type=jnp.float32,
        )

    logp = expo_ref[...]
    peak = jnp.max(logp, axis=0, keepdims=True)
    expo = jnp.exp(logp - peak)
    expo_ref[...] = expo
    which = lax.broadcasted_iota(jnp.int32, (8, rows), 0)
    stat_ref[...] = jnp.where(which == 0, peak, jnp.sum(expo, axis=0, keepdims=True))


def insert_kernel(
    every_ref, stat_ref, expo_ref, ins_ref, square_ref, inv_tau_ref, fresh_ref, weight_ref, loglik_ref, turned
):
    rows = expo_ref.shape[1]
    height = expo_ref.shape[0]
    owned = height // ROT
    count = rows // TRANS
    peaks, sums = every_ref[:, 0, :], every_ref[:, 1, :]
    peak = jnp.broadcast_to(jnp.max(peaks, axis=0, keepdims=True), (8, rows))
    top = peak
    for t in range(1, TRANS):
        top = jnp.maximum(top, pltpu.roll(peak, t * count, 1))
    part = jnp.sum(sums * jnp.exp(peaks - top[:1]), axis=0, keepdims=True)
    part = jnp.broadcast_to(part, (8, rows))
    total = part
    for t in range(1, TRANS):
        total = total + pltpu.roll(part, t * count, 1)
    loglik_ref[...] = top + jnp.log(total)
    factor = jnp.exp(stat_ref[:1] - top[:1]) / total[:1]

    summed = jnp.zeros((owned, rows), jnp.float32)
    for r in range(ROT):
        post = (expo_ref[r * owned : (r + 1) * owned] * factor).astype(jnp.bfloat16)
        summed = summed + post.astype(jnp.float32)
        first = (ROT - r) % ROT
        for spot in (first, first + ROT):
            turned[spot * owned : (spot + 1) * owned] = post
    weight_ref[...] = jnp.broadcast_to(jnp.sum(summed, axis=1, keepdims=True), weight_ref.shape)
    denom = jnp.dot(summed, square_ref[...], precision=HIGH, preferred_element_type=jnp.float32)
    inverse = 1.0 / (denom + inv_tau_ref[...])
    inverse = jnp.concatenate([inverse, inverse], axis=1)

    fresh_ref[...] = jnp.zeros_like(fresh_ref)

    @pl.loop(0, ROT // BATCH)
    def _(batch):
        left, right = [], []
        for part_index in range(BATCH):
            s = batch * BATCH + part_index
            start = pl.multiple_of((ROT - s) * owned, owned)
            left.append(turned[pl.ds(start, height), :])
            right.append(ins_ref[s])
        fresh_ref[...] += jnp.dot(
            jnp.concatenate(left, axis=1), jnp.concatenate(right, axis=0),
            preferred_element_type=jnp.float32,
        )

    for b in range(ROT):
        block = pl.ds(b * owned, owned)
        fresh_ref[block] = fresh_ref[block] * inverse


def per_device(
    images, references, class_logprior, ctf_table, noise_power, tau_power, defocus, offsets
):
    n = lax.axis_size("img")
    local = images.shape[0]
    count = local * n
    rows = count * TRANS
    owned_true = references.shape[0]
    owned = -(-owned_true // 16) * 16
    spare = owned - owned_true
    vmem = pl.BlockSpec(memory_space=pltpu.VMEM)
    limit = 60 * 1024 * 1024

    moves = offsets.astype(jnp.float32)
    meta = jnp.concatenate(
        [defocus.astype(jnp.float32)[:, None], moves[..., 0], moves[..., 1]], axis=1
    )
    meta = jnp.pad(meta, ((0, 0), (0, LANES - meta.shape[1]))).astype(jnp.bfloat16)
    own = jnp.concatenate([turn_major(images), meta[None]], axis=0)
    gathered = gather_images(own, n)
    refs = jnp.pad(turn_major(references), ((0, 0), (0, spare), (0, 0)))
    prior = jnp.pad(class_logprior.astype(jnp.float32), (0, spare), constant_values=-1e30)
    prior = jnp.broadcast_to(prior[:, None], (owned, 128))

    inserted, expo, stat, square = pl.pallas_call(
        score_kernel,
        out_shape=(
            jax.ShapeDtypeStruct((ROT, rows, LANES), jnp.bfloat16),
            jax.ShapeDtypeStruct((ROT * owned, rows), jnp.float32),
            jax.ShapeDtypeStruct((8, rows), jnp.float32),
            jax.ShapeDtypeStruct((rows, HALF), jnp.float32),
        ),
        in_specs=[vmem] * 6,
        out_specs=(vmem,) * 4,
        scratch_shapes=[pltpu.VMEM((2 * ROT * owned, LANES), jnp.bfloat16)],
        compiler_params=pltpu.CompilerParams(vmem_limit_bytes=limit),
        name="score",
    )(
        gathered,
        refs,
        prior,
        jnp.tile(ctf_table, (1, STRIDE)),
        jnp.tile(noise_power, STRIDE)[None],
        jnp.asarray(phase_rows()),
    )
    every = exchange_stats(stat, n, lax.axis_size("cls")).reshape(-1, 8, rows)
    fresh, weight, loglik = pl.pallas_call(
        insert_kernel,
        out_shape=(
            jax.ShapeDtypeStruct((ROT * owned, LANES), jnp.float32),
            jax.ShapeDtypeStruct((owned, 128), jnp.float32),
            jax.ShapeDtypeStruct((8, rows), jnp.float32),
        ),
        in_specs=[vmem] * 6,
        out_specs=(vmem,) * 3,
        scratch_shapes=[pltpu.VMEM((2 * ROT * owned, rows), jnp.bfloat16)],
        compiler_params=pltpu.CompilerParams(vmem_limit_bytes=limit),
        name="insert",
    )(every, stat, expo, inserted, square, jnp.tile(1.0 / tau_power, STRIDE)[None])
    fresh = fresh.reshape(ROT, owned, 2, STRIDE, CYCLES)[:, :owned_true]
    fresh = fresh.transpose(1, 2, 4, 0, 3).reshape(owned_true, 2 * CYCLES * ANG)
    mine = lax.dynamic_slice_in_dim(loglik[0], lax.axis_index("img") * local, local, 0)
    return fresh, weight[:owned_true, 0] / count, mine


def solution(mesh):
    return jax.shard_map(
        per_device,
        mesh=mesh,
        in_specs=(
            P("img", None),
            P(("img", "cls"), None),
            P(("img", "cls")),
            P(),
            P(),
            P(),
            P("img"),
            P("img", None, None),
        ),
        out_specs=(P(("img", "cls"), None), P(("img", "cls")), P("img")),
        check_vma=False,
    )
```

profile of v0, /device:TPU:0, one launch (start us, length us, event | category | flops | bytes accessed | tf_op | source)
XLA Modules:
  0.0 80.4 jit_solution(10324528847084417270)
XLA Ops:
  0.6 0.7 broadcast_divide_fusion
  1.3 0.7 convert_bitcast_fusion
  2.0 0.1 copy.20
  2.1 0.6 broadcast_in_dim_tile.7.inv_tau_ref
  2.7 0.7 tile.10
  3.3 0.6 broadcast_in_dim_tile.6.noise_ref
  3.9 0.7 convert_convert_fusion
  4.6 0.1 copy.27
  4.7 0.1 copy.28
  4.8 0.1 fusion.5
  4.9 1.3 %broadcast_in_dim.15.prior_ref = f32[16,128]{1,0:T(8,128)} broadcast(bf16[16]{0:T(256)(128)(2,1)} %param.11), dimensions={0} | broadcast | bytes 8224 | tf_op jit(solution)/shard_map/broadcast_in_dim | solution.py:330
  6.2 0.7 tile.8
  6.9 0.7 tile.9.ctf_ref
  7.6 2.0 %copy.18 = bf16[8,9216]{0,1:T(8,128)(2,1)S(1)} copy(bf16[8,9216]{1,0:T(8,128)(2,1)} %param.9) | data formatting | bytes 294912 | tf_op args[0]
  9.5 0.0 copy-start
  9.5 1.3 %copy.19 = bf16[36,8,2,4,32]{4,3,2,1,0:T(4,128)(2,1)S(1)} copy(bf16[36,8,2,4,32]{1,3,0,4,2:T(4,128)(2,1)S(1)} %bitcast.19) | data formatting | bytes 294912 | tf_op jit(solution)/shard_map/transpose | solution.py:51
  10.9 0.4 reshape.38
  11.3 0.7 pad_maximum_fusion.refs_0_
  12.0 14.7 %gather_images.1.images_ref = bf16[8,37,8,256]{3,2,1,0:T(8,128)(2,1)} custom-call(bf16[37,8,256]{2,1,0:T(8,128)(2,1)} %pad_maximum_fusion.refs_0_), custom_call_target="tpu_custom_call" | custom-call | tf_op jit(solution)/shard_map/gather_images/pallas_call | solution.py:97
  26.7 0.0 copy-done
  26.7 1.1 %copy.23 = bf16[16,9216]{0,1:T(8,128)(2,1)S(1)} copy(bf16[16,9216]{1,0:T(8,128)(2,1)S(1)} %copy-done) | data formatting | bytes 589824 | tf_op args[1]
  27.8 4.5 %copy.24 = bf16[36,16,2,4,32]{4,3,2,1,0:T(4,128)(2,1)S(1)} copy(bf16[36,16,2,4,32]{1,3,0,4,2:T(4,128)(2,1)S(1)} %bitcast.20) | data formatting | bytes 589824 | tf_op jit(solution)/shard_map/transpose | solution.py:51
  32.4 1.6 %reshape.40.refs_ref = bf16[36,16,256]{2,1,0:T(8,128)(2,1)} reshape(bf16[36,16,2,4,32]{4,3,2,1,0:T(4,128)(2,1)S(1)} %copy.24) | data formatting | bytes 589824 | tf_op jit(solution)/shard_map/reshape | solution.py:51
  33.9 11.6 %score.1 = (bf16[36,256,256]{2,1,0:T(8,128)(2,1)}, f32[576,256]{1,0:T(8,128)}, f32[8,256]{1,0:T(8,128)}, f32[256,128]{1,0:T(8,128)}) custom-call(bf16[8,37,8,256]{3,2,1,0:T(8,128)(2,1)} %gather_images.1.images_ref, bf16[36,16,256]{2,1,0:T(8,128)(2,1)} %reshape.40.refs_ref, f32[16,128]{1,0:T(8,128)} %broadcast_in_dim.15.prior_ref, f32[16,128]{1,0:T(8,128)} %tile.9.ctf_ref, ...), custom_call_target="tpu_custom_call" | custom-call | tf_op jit(solution)/shard_map/score/pallas_call | solution.py:332
  45.6 12.4 %exchange_stats.1 = f32[8,4,8,256]{3,2,1,0:T(8,128)} custom-call(f32[8,256]{1,0:T(8,128)} %get-tuple-element.10.refs_0_.stat_ref), custom_call_target="tpu_custom_call" | custom-call | tf_op jit(solution)/shard_map/exchange_stats/pallas_call | solution.py:153
  58.0 8.3 %insert.1 = (f32[576,256]{1,0:T(8,128)}, f32[16,128]{1,0:T(8,128)}, f32[8,256]{1,0:T(8,128)}) custom-call(f32[32,8,256]{2,1,0:T(8,128)} %bitcast.21, f32[8,256]{1,0:T(8,128)} %get-tuple-element.10.refs_0_.stat_ref, f32[576,256]{1,0:T(8,128)} %get-tuple-element.11.expo_ref, bf16[36,256,256]{2,1,0:T(8,128)(2,1)} %get-tuple-element.12.ins_ref, ...), custom_call_target="tpu_custom_call" | custom-call | tf_op jit(solution)/shard_map/insert/pallas_call | solution.py:354
  66.2 1.3 %multiply_reduce_fusion = f32[16]{0:T(128)} fusion(f32[16,128]{1,0:T(8,128)} %get-tuple-element.15), kind=kLoop, calls=%fused_computation.5 | loop fusion | flops 16 | bytes 128 | tf_op jit(solution)/shard_map/div | solution.py:370
  67.6 0.7 slice.17
  68.3 0.6 dynamic-slice_bitcast_fusion
  68.8 2.2 %reshape.42 = f32[36,16,2,4,32]{4,3,2,1,0:T(4,128)S(1)} reshape(f32[576,256]{1,0:T(8,128)} %get-tuple-element.14) | data formatting | bytes 1179648 | tf_op jit(solution)/shard_map/reshape | solution.py:367
  71.1 5.6 %copy.25 = f32[16,2,32,36,4]{0,4,3,2,1:T(4,128)} copy(f32[16,2,32,36,4]{2,4,1,0,3:T(4,128)S(1)} %bitcast.18) | data formatting | bytes 1179648 | tf_op jit(solution)/shard_map/transpose | solution.py:368
  76.7 3.7 %copy.26 = f32[16,9216]{1,0:T(8,128)} copy(f32[16,9216]{0,1:T(8,128)} %bitcast.17) | data formatting | bytes 1179648
  (2 shorter events, 0.0 us)
Async XLA Ops:
  9.5 17.2 %copy-start = (bf16[16,9216]{1,0:T(8,128)(2,1)S(1)}, bf16[16,9216]{1,0:T(8,128)(2,1)}, u32[]{:S(2)}) copy-start(bf16[16,9216]{1,0:T(8,128)(2,1)} %param.10) | copy-start | bytes 884740
where the time goes:
time: 80.9 us; the launch traced here: 80.4 us
  Pallas kernels  47 us (58%)
  local copies, waits for them, and re-layouts  28.6 us (35%)
  other arithmetic  4.09 us (5%)
    pallas_call x1, Pallas kernels, gather_images(): pl.pallas_call(lambda *refs: gather_kernel(n, *refs), out_shape=jax.Shape...  14.7 us
    pallas_call x1, Pallas kernels, exchange_stats(): pl.pallas_call(lambda *refs: exchange_kernel(n, m, *refs), out_shape=jax....  12.4 us
    pallas_call x1, Pallas kernels, per_device(): pl.pallas_call(score_kernel, out_shape=(jax.ShapeDtypeStruct((ROT, rows,...  11.6 us
    pallas_call x1, Pallas kernels, per_device(): pl.pallas_call(insert_kernel, out_shape=(jax.ShapeDtypeStruct((ROT * owne...  8.29 us
    unnamed x5, local copies, waits for them, and re-layouts  6.82 us
    transpose x2, local copies, waits for them, and re-layouts, turn_major(): return shaped.transpose(3, 0, 1, 4, 2).reshape(ROT, source.shape[0], LANES)  5.88 us
    transpose x1, local copies, waits for them, and re-layouts, per_device(): fresh = fresh.transpose(1, 2, 4, 0, 3).reshape(owned_true, 2 * CYCLES * ANG)  5.61 us
    reshape x1, local copies, waits for them, and re-layouts, per_device(): fresh = fresh.reshape(ROT, owned, 2, STRIDE, CYCLES)[:, :owned_true]  2.21 us

commit v1 on v0

v1 whole, which is shorter than its diff:
```python
import math

import jax
import jax.numpy as jnp
import numpy as np
from jax import lax
from jax.experimental import pallas as pl
from jax.experimental.pallas import tpu as pltpu
from jax.sharding import PartitionSpec as P

TRANS = 4
CYCLES = 32
ANG = 144
ROT = 36
NDEF = 16

STRIDE = ANG // ROT
REACH = 3
SIDE = 2 * REACH + 1
COMBOS = SIDE * SIDE
TABLE_ROWS = 112
HIGH = lax.Precision.HIGHEST
offset_sigma = 2.0

LANE = 128
LOW = 8
GROUPS = CYCLES // LOW
SPAN = LOW * ANG
COLS = SPAN // LANE
MIX = ROT // COLS
TURN = LANE // MIX
SEG = LANE // LOW
TILES = GROUPS * COLS
WIDE = 2 * LANE
BY_LANE = (((1,), (1,)), ((), ()))
F32 = jnp.float32
BF16 = jnp.bfloat16


def phase_rows():
    group = np.arange(GROUPS)[:, None, None]
    column = np.arange(COLS)[None, :, None]
    lane = np.arange(LANE)[None, None, :]
    radius = group * LOW + lane % LOW + 1.0
    theta = 2.0 * math.pi * (column * SEG + lane // LOW) / ANG
    freq_x = (radius * np.cos(theta)).reshape(TILES, 1, LANE)
    freq_y = (radius * np.sin(theta)).reshape(TILES, 1, LANE)
    combo = np.arange(COMBOS)[None, :, None]
    dx = combo // SIDE - REACH
    dy = combo % SIDE - REACH
    angle = -2.0 * math.pi * (dx * freq_x + dy * freq_y) / (2.0 * CYCLES)
    full = np.concatenate([np.cos(angle), np.sin(angle)], axis=2)
    high = full.astype(jnp.bfloat16)
    low = (full - high.astype(np.float64)).astype(jnp.bfloat16)
    table = np.zeros((TILES, TABLE_ROWS, WIDE), jnp.bfloat16)
    table[:, :COMBOS] = high
    table[:, COMBOS : 2 * COMBOS] = low
    return table


def iota(shape, dim):
    return lax.broadcasted_iota(jnp.int32, shape, dim)


def onehot(mask):
    return jnp.where(mask, 1.0, 0.0).astype(F32)


def column_of(row, size):
    square = jnp.broadcast_to(row, (size, size))
    return jnp.sum(
        jnp.where(iota((size, size), 0) == iota((size, size), 1), square, 0.0), axis=1, keepdims=True
    )


def pick_segments(sources, seg):
    value = sources[0]
    for s in range(1, LOW):
        value = jnp.where(seg == s, sources[s], value)
    return value


def natural_to_mixed(block, j, seg):
    sources = []
    for s in range(LOW):
        cycle = (s - j) % LOW
        n = (cycle * COLS + j - s) // LOW
        sources.append(block(n))
    return pick_segments(sources, seg)


def kernel(
    n, m,
    images_hbm, refs_hbm, prior_ref, ctf_ref, noise_ref, tau_ref, defocus_ref, offsets_ref, table_hbm,
    fresh_ref, weight_ref, loglik_ref,
    images_nat, refs_nat, table, own, every, spin, blend, unblend, turned, weighted_a, weighted_b, inserted,
    acc, post, mixed, stat, stats,
    load_sem, left_sem, direct_sem, relay_left, relay_sem, cls_left, cls_sem, img_left, img_sem, keep_sem,
):
    local = images_nat.shape[0]
    owned = refs_nat.shape[0]
    count = n * local
    rows = count * TRANS
    width = stat.shape[1]
    height = ROT * owned
    step = MIX * owned
    weighted = (weighted_a, weighted_b)

    row_id, column_id = lax.axis_index("img"), lax.axis_index("cls")
    partner = row_id + 1 - 2 * lax.rem(row_id, 2)
    peers = [lax.rem(row_id + 2 * hop, n) for hop in range(1, n // 2)]
    above = [{"cls": lax.rem(column_id + hop, m)} for hop in range(1, m)]
    beside = [{"img": lax.rem(row_id + hop, n)} for hop in range(1, n)]

    loads = [
        pltpu.make_async_copy(images_hbm, images_nat, load_sem.at[0]),
        pltpu.make_async_copy(refs_hbm, refs_nat, load_sem.at[1]),
        pltpu.make_async_copy(table_hbm, table, load_sem.at[2]),
    ]
    for copy in loads:
        copy.start()
    barrier = pltpu.get_barrier_semaphore()
    for peer in above + beside:
        pl.semaphore_signal(barrier, inc=1, device_id=peer, device_id_type=pl.DeviceIdType.MESH)

    def send(src, dst, peer, left, landed):
        copy = pltpu.make_async_remote_copy(
            src_ref=src, dst_ref=dst, send_sem=left, recv_sem=landed,
            device_id=peer, device_id_type=pl.DeviceIdType.MESH,
        )
        copy.start()
        return copy

    source = iota((LANE, LANE), 0)
    target = iota((LANE, LANE), 1)
    for j in range(LOW):
        place = (source % SEG) * LOW + (source // SEG + (LOW - j)) % LOW
        blend[j] = onehot(target == place).astype(BF16)
        place = (target % SEG) * LOW + (target // SEG + (LOW - j)) % LOW
        back = onehot(source == place).astype(BF16)
        unblend[j, :LANE] = back
        unblend[j, LANE:] = back

    meta = jnp.zeros((local, WIDE), F32)
    lane = iota((local, WIDE), 1)
    meta = jnp.where(lane == 0, column_of(defocus_ref[...].astype(F32), local), meta)
    for t in range(TRANS):
        for axis in range(2):
            value = column_of(offsets_ref[t, axis : axis + 1].astype(F32), local)
            meta = jnp.where(lane == 1 + t + axis * TRANS, value, meta)
    own[0] = meta.astype(BF16)

    def mix(nat, size, j):
        seg = iota((size, LANE), 1) // SEG
        parts = []
        for g in range(GROUPS):
            for p in range(2):
                start = p * CYCLES * ANG + g * SPAN

                def block(k, start=start):
                    return nat[:, start + k * LANE : start + (k + 1) * LANE].astype(F32)

                parts.append(natural_to_mixed(block, j, seg))
        stacked = jnp.concatenate(parts, axis=0).astype(BF16)
        return jnp.dot(stacked, blend[j % LOW], preferred_element_type=F32)

    loads[0].wait()
    for j in range(COLS):
        moved = mix(images_nat, local, j).astype(BF16)
        for g in range(GROUPS):
            for p in range(2):
                index = g * 2 + p
                own[1 + g * COLS + j, :, p * LANE : (p + 1) * LANE] = moved[
                    index * local : (index + 1) * local
                ]

    pl.semaphore_wait(barrier, n + m - 2)

    def part_of(g):
        return pl.ds(0, COLS + 1) if g == 0 else pl.ds(1 + g * COLS, COLS)

    direct = [[None] * len(peers) for _ in range(GROUPS)]
    relays = [[None] * (len(peers) + 1) for _ in range(GROUPS)]
    for g in range(GROUPS):
        piece = part_of(g)
        for hop, peer in enumerate(peers):
            direct[g][hop] = send(
                own.at[piece], every.at[row_id, piece], {"img": peer}, left_sem.at[g, hop], direct_sem.at[g, hop]
            )
        relays[g][0] = send(
            own.at[piece], every.at[row_id, piece], {"img": partner}, relay_left.at[g, 0], relay_sem.at[g, 0]
        )
    keep = pltpu.make_async_copy(own, every.at[row_id], keep_sem.at[0])
    keep.start()

    loads[1].wait()
    for j in range(COLS):
        spin[j] = mix(refs_nat, owned, j)
    lane = iota((2 * GROUPS * owned, LANE), 1)
    for q in range(MIX):
        before = pltpu.roll(spin[COLS - 1], q * TURN, 1) if q else None
        for j in range(COLS):
            if q:
                here = pltpu.roll(spin[j], q * TURN, 1)
                value = jnp.where(lane < q * TURN, before, here).astype(BF16)
                before = here
            else:
                value = spin[j].astype(BF16)
            for g in range(GROUPS):
                for p in range(2):
                    index = g * 2 + p
                    for spot in ((COLS - j) % COLS, (COLS - j) % COLS + COLS):
                        turned[
                            g, spot * step + q * owned : spot * step + (q + 1) * owned, p * LANE : (p + 1) * LANE
                        ] = value[index * owned : (index + 1) * owned]
    power = [jnp.zeros((owned, LANE), F32) for _ in range(GROUPS)]
    for j in range(COLS):
        for g in range(GROUPS):
            for p in range(2):
                index = g * 2 + p
                entry = spin[j, index * owned : (index + 1) * owned]
                power[g] = power[g] + entry * entry
    power = jnp.concatenate(power, axis=1)
    spread = onehot(
        iota((CYCLES, GROUPS * LANE), 0)
        == iota((CYCLES, GROUPS * LANE), 1) // LANE * LOW + iota((CYCLES, GROUPS * LANE), 1) % LOW
    )

    def widen(value):
        return jnp.dot(value, spread, precision=HIGH, preferred_element_type=F32)

    ctf_wide = widen(ctf_ref[...])
    noise_wide = widen(jnp.broadcast_to(noise_ref[...], (8, CYCLES)))[:1]
    tau_wide = widen(jnp.broadcast_to(1.0 / tau_ref[...], (8, CYCLES)))[:1]
    prior = column_of(prior_ref[...].astype(F32), owned)

    def arrive(g):
        piece = part_of(g)
        for hop, copy in enumerate(direct[g]):
            copy.wait_recv()
            origin = lax.rem(row_id + n - 2 * (hop + 1), n)
            slot = every.at[origin, piece]
            relays[g][hop + 1] = send(
                slot, slot, {"img": partner}, relay_left.at[g, hop + 1], relay_sem.at[g, hop + 1]
            )

    def settle(g):
        for copy in relays[g]:
            copy.wait_recv()

    def setup():
        meta = every[:, 0].astype(F32).reshape(count, WIDE)
        group = iota((count, NDEF), 1).astype(F32)
        chosen = onehot(group == meta[:, :1])
        contrast = jnp.dot(chosen, ctf_wide, precision=HIGH, preferred_element_type=F32)
        square = contrast * contrast
        spot = iota((count, TABLE_ROWS), 1).astype(F32)
        lane = iota((count, LANE), 1)
        picks, terms = [], []
        for t in range(TRANS):
            dx = meta[:, 1 + t : 2 + t]
            dy = meta[:, 1 + TRANS + t : 2 + TRANS + t]
            index = (dx + REACH) * SIDE + (dy + REACH)
            picks.append(onehot((spot == index) | (spot == index + COMBOS)).astype(BF16))
            value = -(dx * dx + dy * dy) / (2.0 * offset_sigma * offset_sigma)
            terms.append(jnp.where(lane == 0, value, 0.0))
        coef = square / (2.0 * noise_wide)
        coef = jnp.concatenate([coef] * TRANS, axis=0)
        base = prior - lax.dot_general(power, coef, BY_LANE, precision=HIGH, preferred_element_type=F32)
        base = base + lax.dot_general(
            jnp.ones((owned, LANE), F32), jnp.concatenate(terms, axis=0), BY_LANE,
            precision=HIGH, preferred_element_type=F32,
        )
        return picks, contrast, square, contrast / noise_wide, base

    def build(g, picks, contrast, scaled, slot):
        bright = contrast[:, g * LANE : (g + 1) * LANE]
        scale = scaled[:, g * LANE : (g + 1) * LANE]
        for j in range(COLS):
            tile = g * COLS + j
            picture = every[:, 1 + tile].astype(F32).reshape(count, WIDE)
            real, imag = picture[:, :LANE], picture[:, LANE:]
            for t in range(TRANS):
                phase = jnp.dot(picks[t], table[tile], preferred_element_type=F32)
                cosine, sine = phase[:, :LANE], phase[:, LANE:]
                moved_real = real * cosine - imag * sine
                moved_imag = real * sine + imag * cosine
                span = slice(t * count, (t + 1) * count)
                inserted[tile, span, :LANE] = (moved_real * bright).astype(BF16)
                inserted[tile, span, LANE:] = (moved_imag * bright).astype(BF16)
                slot[span, j * WIDE : j * WIDE + LANE] = (moved_real * scale).astype(BF16)
                slot[span, j * WIDE + LANE : (j + 1) * WIDE] = (moved_imag * scale).astype(BF16)

    def score(g, slot):
        left = jnp.concatenate(
            [turned[g, (COLS - j) * step : (COLS - j) * step + height] for j in range(COLS)], axis=1
        )
        value = lax.dot_general(left, slot[...], BY_LANE, preferred_element_type=F32)
        if g == 0:
            acc[...] = value
        else:
            acc[...] += value

    loads[2].wait()
    keep.wait()
    arrive(0)
    settle(0)
    picks, contrast, square, scaled, base = setup()
    for g in range(GROUPS):
        if g + 1 < GROUPS:
            arrive(g + 1)
        if g:
            settle(g)
        build(g, picks, contrast, scaled, weighted[g % 2])
        if g:
            score(g - 1, weighted[(g - 1) % 2])
    score(GROUPS - 1, weighted[(GROUPS - 1) % 2])

    def over_shifts(value, combine):
        total = value
        for t in range(1, TRANS):
            total = combine(total, pltpu.roll(value, t * count, 1))
        return total

    peak = jnp.full((owned, rows), -jnp.inf, F32)
    for r in range(ROT):
        peak = jnp.maximum(peak, acc[r * owned : (r + 1) * owned])
    peak = jnp.max(peak + base, axis=0, keepdims=True)
    peak = over_shifts(jnp.broadcast_to(peak, (8, rows)), jnp.maximum)[:1]
    less = base - peak
    total = jnp.zeros((owned, rows), F32)
    for r in range(ROT):
        expo = jnp.exp(acc[r * owned : (r + 1) * owned] + less)
        acc[r * owned : (r + 1) * owned] = expo
        total = total + expo
    total = jnp.sum(total, axis=0, keepdims=True)
    total = over_shifts(jnp.broadcast_to(total, (8, rows)), jnp.add)[:1]
    stat[0:1] = peak[:, :width]
    stat[1:2] = total[:, :width]

    def send_all(src, dst, targets, left, landed):
        return [send(src, dst, peer, left.at[hop], landed.at[hop]) for hop, peer in enumerate(targets)]

    slot = stats.at[row_id, column_id]
    first = send_all(stat, slot, above, cls_left, cls_sem)
    keep = pltpu.make_async_copy(stat, slot, keep_sem.at[1])
    keep.start()
    keep.wait()
    for copy in first:
        copy.wait_recv()
    second = send_all(stats.at[row_id], stats.at[row_id], beside, img_left, img_sem)
    for copy in second:
        copy.wait_recv()

    entries = [stats[i, c] for i in range(n) for c in range(m)]
    top = entries[0]
    for entry in entries[1:]:
        top = jnp.maximum(top, entry)
    top = top[:1]
    whole = jnp.zeros((1, width), F32)
    for entry in entries:
        whole = whole + entry[1:2] * jnp.exp(entry[:1] - top)
    logs = jnp.broadcast_to(top + jnp.log(whole), (8, width))
    loglik_ref[...] = pltpu.roll(logs, width - row_id * local, 1)[:1, :local]
    factor = jnp.exp(stat[0:1] - top) / whole
    factor = jnp.concatenate([factor] * (rows // width), axis=1)

    summed = jnp.zeros((owned, rows), F32)
    for r in range(ROT):
        value = (acc[r * owned : (r + 1) * owned] * factor).astype(BF16)
        summed = summed + value.astype(F32)
        shift, q = r // MIX, r % MIX
        for spot in ((COLS - shift) % COLS, (COLS - shift) % COLS + COLS):
            post[spot * step + q * owned : spot * step + (q + 1) * owned] = value
    weight = jnp.sum(summed, axis=1, keepdims=True) * (1.0 / count)
    diagonal = iota((owned, owned), 0) == iota((owned, owned), 1)
    weight_ref[...] = jnp.sum(
        jnp.where(diagonal, jnp.broadcast_to(weight, (owned, owned)), 0.0), axis=0, keepdims=True
    )
    denom = jnp.dot(
        summed, jnp.concatenate([square] * TRANS, axis=0), precision=HIGH, preferred_element_type=F32
    )
    inverse = 1.0 / (denom + tau_wide)

    lane = iota((owned, LANE), 1)
    seg = iota((owned, LANE), 1) // SEG
    for g in range(GROUPS):
        left = jnp.concatenate(
            [post[(COLS - s) * step : (COLS - s) * step + height] for s in range(COLS)], axis=1
        )
        right = jnp.concatenate([inserted[g * COLS + s] for s in range(COLS)], axis=0)
        mixed[...] = jnp.dot(left, right, preferred_element_type=F32)
        scale = inverse[:, g * LANE : (g + 1) * LANE]
        spread_out = [[], []]
        for j in range(COLS):
            halves = []
            for p in range(2):
                half = slice(p * LANE, (p + 1) * LANE)
                value = mixed[j * step : j * step + owned, half]
                for q in range(1, MIX):
                    after = (j + 1) % COLS
                    here = pltpu.roll(mixed[j * step + q * owned : j * step + (q + 1) * owned, half], LANE - q * TURN, 1)
                    there = pltpu.roll(
                        mixed[after * step + q * owned : after * step + (q + 1) * owned, half], LANE - q * TURN, 1
                    )
                    value = value + jnp.where(lane < LANE - q * TURN, here, there)
                halves.append(value * scale)
            value = jnp.concatenate(halves, axis=0)
            high = value.astype(BF16)
            low = (value - high.astype(F32)).astype(BF16)
            value = jnp.dot(jnp.concatenate([high, low], axis=1), unblend[j % LOW], preferred_element_type=F32)
            for p in range(2):
                spread_out[p].append(value[p * owned : (p + 1) * owned])
        for p in range(2):
            for k in range(COLS):
                start = p * CYCLES * ANG + g * SPAN + k * LANE
                fresh_ref[:, start : start + LANE] = pick_segments(
                    [spread_out[p][(LOW * k + s) % COLS] for s in range(LOW)], seg
                )

    for copy in sum(direct, []) + sum(relays, []) + first + second:
        copy.wait_send()


def per_device(
    images, references, class_logprior, ctf_table, noise_power, tau_power, defocus, offsets
):
    n, m = lax.axis_size("img"), lax.axis_size("cls")
    local = images.shape[0]
    count = local * n
    rows = count * TRANS
    owned_true = references.shape[0]
    owned = -(-owned_true // 16) * 16
    spare = owned - owned_true
    width = max(count, LANE)
    height = ROT * owned
    vmem = pl.BlockSpec(memory_space=pltpu.VMEM)
    hbm = pl.BlockSpec(memory_space=pl.ANY)
    prior = class_logprior
    if spare:
        references = jnp.pad(references, ((0, spare), (0, 0)))
        prior = jnp.pad(class_logprior.astype(F32), (0, spare), constant_values=-1e30)

    dma = pltpu.SemaphoreType.DMA
    hops = n // 2 - 1
    fresh, weight, loglik = pl.pallas_call(
        lambda *refs: kernel(n, m, *refs),
        out_shape=(
            jax.ShapeDtypeStruct((owned, 2 * CYCLES * ANG), F32),
            jax.ShapeDtypeStruct((1, owned), F32),
            jax.ShapeDtypeStruct((1, local), F32),
        ),
        in_specs=[hbm, hbm] + [vmem] * 6 + [hbm],
        out_specs=(vmem,) * 3,
        scratch_shapes=[
            pltpu.VMEM((local, 2 * CYCLES * ANG), BF16),
            pltpu.VMEM((owned, 2 * CYCLES * ANG), BF16),
            pltpu.VMEM((TILES, TABLE_ROWS, WIDE), BF16),
            pltpu.VMEM((1 + TILES, local, WIDE), BF16),
            pltpu.VMEM((n, 1 + TILES, local, WIDE), BF16),
            pltpu.VMEM((COLS, 2 * GROUPS * owned, LANE), F32),
            pltpu.VMEM((LOW, LANE, LANE), BF16),
            pltpu.VMEM((LOW, WIDE, LANE), BF16),
            pltpu.VMEM((GROUPS, 2 * height, WIDE), BF16),
            pltpu.VMEM((rows, COLS * WIDE), BF16),
            pltpu.VMEM((rows, COLS * WIDE), BF16),
            pltpu.VMEM((TILES, rows, WIDE), BF16),
            pltpu.VMEM((height, rows), F32),
            pltpu.VMEM((2 * height, rows), BF16),
            pltpu.VMEM((height, WIDE), F32),
            pltpu.VMEM((2, width), F32),
            pltpu.VMEM((n, m, 2, width), F32),
            dma((3,)),
            dma((GROUPS, hops)),
            dma((GROUPS, hops)),
            dma((GROUPS, hops + 1)),
            dma((GROUPS, hops + 1)),
            dma((m - 1,)),
            dma((m - 1,)),
            dma((n - 1,)),
            dma((n - 1,)),
            dma((2,)),
        ],
        compiler_params=pltpu.CompilerParams(
            collective_id=0, has_side_effects=True, vmem_limit_bytes=60 * 1024 * 1024
        ),
        name="classify",
    )(
        images,
        references,
        prior[None],
        ctf_table,
        noise_power[None],
        tau_power[None],
        defocus[None],
        offsets.transpose(1, 2, 0),
        jnp.asarray(phase_rows()),
    )
    return fresh[:owned_true], weight[0, :owned_true], loglik[0]


def solution(mesh):
    return jax.shard_map(
        per_device,
        mesh=mesh,
        in_specs=(
            P("img", None),
            P(("img", "cls"), None),
            P(("img", "cls")),
            P(),
            P(),
            P(),
            P("img"),
            P("img", None, None),
        ),
        out_specs=(P(("img", "cls"), None), P(("img", "cls")), P("img")),
        check_vma=False,
    )
```

time: 80.9 us -> 41.1 us (0.51)
  local copies, waits for them, and re-layouts: 28.6 us -> 4.26 us
  Pallas kernels: 47 us -> 35.9 us
  other arithmetic: 4.09 us -> 0 us
    transpose x3 -> x0, local copies, waits for them, and re-layouts: 11.5 us -> none  [the longest x2 5.88 us: turn_major(): return shaped.transpose(3, 0, 1, 4, 2).reshape(ROT, source.shape[0], LANES)]
    pallas_call x4 -> x1, Pallas kernels: 47 us -> 35.9 us  [per_device(): pl.pallas_call(lambda *refs: kernel(n, m, *refs), out_shape=(jax.ShapeDty...]
    reshape x3 -> x0, local copies, waits for them, and re-layouts: 4.15 us -> none  [the longest x1 2.21 us: per_device(): fresh = fresh.reshape(ROT, owned, 2, STRIDE, CYCLES)[:, :owned_true]]
    another operation x6 -> x0, local copies, waits for them, and re-layouts: 3.22 us -> none  [the longest x2 1.38 us: per_device(): jnp.tile(ctf_table, (1, STRIDE))]
    unnamed x5 -> x3, local copies, waits for them, and re-layouts: 6.82 us -> 4.26 us
    div x2 -> x0, other arithmetic: 1.98 us -> none  [the longest x1 1.32 us: per_device(): return (fresh, weight[:owned_true, 0] / count, mine)]
    broadcast_in_dim x2 -> x0, local copies, waits for them, and re-layouts: 1.42 us -> none  [the longest x1 1.32 us: per_device(): prior = jnp.broadcast_to(prior[:, None], (owned, 128))]
where the time goes in v1:
time: 41.1 us; the launch traced here: 40.8 us
  Pallas kernels  35.9 us (87%)
  local copies, waits for them, and re-layouts  4.26 us (10%)
  between operations  0.64 us (2%)
    pallas_call x1, Pallas kernels, per_device(): pl.pallas_call(lambda *refs: kernel(n, m, *refs), out_shape=(jax.ShapeDty...  35.9 us
    unnamed x3, local copies, waits for them, and re-layouts  4.26 us

profile of v1, /device:TPU:0, one launch (start us, length us, event | category | flops | bytes accessed | tf_op | source)
XLA Modules:
  0.0 40.8 jit_solution(17788479217094173526)
XLA Ops:
  0.6 35.9 %classify.1 = (f32[16,9216]{1,0:T(8,128)}, f32[1,16]{1,0:T(1,128)}, f32[1,8]{1,0:T(1,128)}) custom-call(bf16[8,9216]{1,0:T(8,128)(2,1)} %refs_0_.1, bf16[16,9216]{1,0:T(8,128)(2,1)} %refs_1_.1, bf16[1,16]{1,0:T(2,128)(2,1)} %bitcast.8, f32[16,32]{1,0:T(8,128)} %refs_3_.1, f32[1,32]{1,0:T(1,128)} %bitcast.9, f32[1,32]{1,0:T(1,128)} %bitcast.10, ...), custom_call_target="tpu_custom_call" | custom-call | tf_op jit(solution)/shard_map/classify/pallas_call | solution.py:446
  36.5 1.9 %copy.15 = f32[16,9216]{1,0:T(8,128)} copy(f32[16,9216]{1,0:T(8,128)} %get-tuple-element.12) | data formatting | bytes 1179648
  38.5 1.2 %copy.16 = f32[16]{0:T(128)} copy(f32[16]{0:T(128)} %bitcast.13) | data formatting | bytes 128
  39.6 1.2 %copy.17 = f32[8]{0:T(128)} copy(f32[8]{0:T(128)} %bitcast.12) | data formatting | bytes 64

commit v2 on v1

--- a/solution.py
+++ b/solution.py
@@ -94,8 +94,8 @@
     images_hbm, refs_hbm, prior_ref, ctf_ref, noise_ref, tau_ref, defocus_ref, offsets_ref, table_hbm,
     fresh_ref, weight_ref, loglik_ref,
     images_nat, refs_nat, table, own, every, spin, blend, unblend, turned, weighted_a, weighted_b, inserted,
-    acc, post, mixed, stat, stats,
-    load_sem, left_sem, direct_sem, relay_left, relay_sem, cls_left, cls_sem, img_left, img_sem, keep_sem,
+    acc, post, mixed, scales, stat, stats,
+    load_sem, left_sem, direct_sem, relay_left, relay_sem, stat_left, stat_sem, keep_sem, plane_sem,
 ):
     local = images_nat.shape[0]
     owned = refs_nat.shape[0]
@@ -111,6 +111,10 @@
     peers = [lax.rem(row_id + 2 * hop, n) for hop in range(1, n // 2)]
     above = [{"cls": lax.rem(column_id + hop, m)} for hop in range(1, m)]
     beside = [{"img": lax.rem(row_id + hop, n)} for hop in range(1, n)]
+    others = [
+        {"img": lax.rem(row_id + i, n), "cls": lax.rem(column_id + c, m)}
+        for i in range(n) for c in range(m) if i or c
+    ]
 
     loads = [
         pltpu.make_async_copy(images_hbm, images_nat, load_sem.at[0]),
@@ -175,6 +179,8 @@
                 ]
 
     pl.semaphore_wait(barrier, n + m - 2)
+    for peer in above:
+        pl.semaphore_signal(plane_sem, inc=1, device_id=peer, device_id_type=pl.DeviceIdType.MESH)
 
     def part_of(g):
         return pl.ds(0, COLS + 1) if g == 0 else pl.ds(1 + g * COLS, COLS)
@@ -338,18 +344,13 @@
     stat[0:1] = peak[:, :width]
     stat[1:2] = total[:, :width]
 
-    def send_all(src, dst, targets, left, landed):
-        return [send(src, dst, peer, left.at[hop], landed.at[hop]) for hop, peer in enumerate(targets)]
-
+    stats[row_id, column_id] = stat[...]
+    pl.semaphore_wait(plane_sem, m - 1)
     slot = stats.at[row_id, column_id]
-    first = send_all(stat, slot, above, cls_left, cls_sem)
-    keep = pltpu.make_async_copy(stat, slot, keep_sem.at[1])
-    keep.start()
-    keep.wait()
-    for copy in first:
-        copy.wait_recv()
-    second = send_all(stats.at[row_id], stats.at[row_id], beside, img_left, img_sem)
-    for copy in second:
+    shared = [
+        send(stat, slot, peer, stat_left.at[k], stat_sem.at[k]) for k, peer in enumerate(others)
+    ]
+    for copy in shared:
         copy.wait_recv()
 
     entries = [stats[i, c] for i in range(n) for c in range(m)]
@@ -385,12 +386,16 @@
     lane = iota((owned, LANE), 1)
     seg = iota((owned, LANE), 1) // SEG
     for g in range(GROUPS):
+        scales[g] = inverse[:, g * LANE : (g + 1) * LANE]
+
+    @pl.loop(0, GROUPS)
+    def _(g):
         left = jnp.concatenate(
             [post[(COLS - s) * step : (COLS - s) * step + height] for s in range(COLS)], axis=1
         )
         right = jnp.concatenate([inserted[g * COLS + s] for s in range(COLS)], axis=0)
         mixed[...] = jnp.dot(left, right, preferred_element_type=F32)
-        scale = inverse[:, g * LANE : (g + 1) * LANE]
+        scale = scales[g]
         spread_out = [[], []]
         for j in range(COLS):
             halves = []
@@ -413,13 +418,21 @@
                 spread_out[p].append(value[p * owned : (p + 1) * owned])
         for p in range(2):
             for k in range(COLS):
-                start = p * CYCLES * ANG + g * SPAN + k * LANE
-                fresh_ref[:, start : start + LANE] = pick_segments(
+                start = pl.multiple_of(g * SPAN + (p * CYCLES * ANG + k * LANE), LANE)
+                fresh_ref[:, pl.ds(start, LANE)] = pick_segments(
                     [spread_out[p][(LOW * k + s) % COLS] for s in range(LOW)], seg
                 )
 
-    for copy in sum(direct, []) + sum(relays, []) + first + second:
+    for copy in sum(direct, []) + sum(relays, []) + shared:
         copy.wait_send()
+
+
+def publish(*refs):
+    copies = [pltpu.make_async_copy(refs[k], refs[3 + k], refs[6].at[k]) for k in range(3)]
+    for copy in copies:
+        copy.start()
+    for copy in copies:
+        copy.wait()
 
 
 def per_device(
@@ -446,9 +459,9 @@
     fresh, weight, loglik = pl.pallas_call(
         lambda *refs: kernel(n, m, *refs),
         out_shape=(
-            jax.ShapeDtypeStruct((owned, 2 * CYCLES * ANG), F32),
-            jax.ShapeDtypeStruct((1, owned), F32),
-            jax.ShapeDtypeStruct((1, local), F32),
+            pltpu.VMEM((owned, 2 * CYCLES * ANG), F32),
+            pltpu.VMEM((1, owned), F32),
+            pltpu.VMEM((1, local), F32),
         ),
         in_specs=[hbm, hbm] + [vmem] * 6 + [hbm],
         out_specs=(vmem,) * 3,
@@ -468,6 +481,7 @@
             pltpu.VMEM((height, rows), F32),
             pltpu.VMEM((2 * height, rows), BF16),
             pltpu.VMEM((height, WIDE), F32),
+            pltpu.VMEM((GROUPS, owned, LANE), F32),
             pltpu.VMEM((2, width), F32),
             pltpu.VMEM((n, m, 2, width), F32),
             dma((3,)),
@@ -475,11 +489,10 @@
             dma((GROUPS, hops)),
             dma((GROUPS, hops + 1)),
             dma((GROUPS, hops + 1)),
-            dma((m - 1,)),
-            dma((m - 1,)),
-            dma((n - 1,)),
-            dma((n - 1,)),
-            dma((2,)),
+            dma((n * m - 1,)),
+            dma((n * m - 1,)),
+            dma((1,)),
+            pltpu.SemaphoreType.REGULAR,
         ],
         compiler_params=pltpu.CompilerParams(
             collective_id=0, has_side_effects=True, vmem_limit_bytes=60 * 1024 * 1024
@@ -496,6 +509,16 @@
         offsets.transpose(1, 2, 0),
         jnp.asarray(phase_rows()),
     )
+    shapes = (fresh.shape, weight.shape, loglik.shape)
+    fresh, weight, loglik = pl.pallas_call(
+        publish,
+        out_shape=tuple(jax.ShapeDtypeStruct(shape, F32) for shape in shapes),
+        in_specs=[vmem] * 3,
+        out_specs=(hbm,) * 3,
+        scratch_shapes=[dma((3,))],
+        compiler_params=pltpu.CompilerParams(vmem_limit_bytes=1024 * 1024),
+        name="publish",
+    )(fresh, weight, loglik)
     return fresh[:owned_true], weight[0, :owned_true], loglik[0]
 
 

time: 41.1 us -> 33.7 us (0.82)
  local copies, waits for them, and re-layouts: 4.26 us -> 0 us
  Pallas kernels: 35.9 us -> 32.8 us
    unnamed x3 -> x0, local copies, waits for them, and re-layouts: 4.26 us -> none
    pallas_call x1 -> x2, Pallas kernels: 35.9 us -> 32.8 us  [the longest x1 32 us: per_device(): pl.pallas_call(lambda *refs: kernel(n, m, *refs), out_shape=(pltpu.VMEM((...]
where the time goes in v2:
time: 33.7 us; the launch traced here: 33.5 us
  Pallas kernels  32.8 us (97%)
  between operations  0.64 us (2%)
    pallas_call x1, Pallas kernels, per_device(): pl.pallas_call(lambda *refs: kernel(n, m, *refs), out_shape=(pltpu.VMEM((...  32 us
    pallas_call x1, Pallas kernels, per_device(): pl.pallas_call(publish, out_shape=tuple((jax.ShapeDtypeStruct(shape, F32)...  0.85 us

profile of v2, /device:TPU:0, one launch (start us, length us, event | category | flops | bytes accessed | tf_op | source)
XLA Modules:
  0.0 33.5 jit_solution(16927493075228674672)
XLA Ops:
  0.6 32.0 %classify.1 = (f32[16,9216]{1,0:T(8,128)S(1)}, f32[1,16]{1,0:T(1,128)S(1)}, f32[1,8]{1,0:T(1,128)S(1)}) custom-call(bf16[8,9216]{1,0:T(8,128)(2,1)} %refs_0_.1, bf16[16,9216]{1,0:T(8,128)(2,1)} %refs_1_.1, bf16[1,16]{1,0:T(2,128)(2,1)} %bitcast.8, f32[16,32]{1,0:T(8,128)} %refs_3_.1, f32[1,32]{1,0:T(1,128)} %bitcast.9, f32[1,32]{1,0:T(1,128)} %bitcast.10, ...), custom_call_target="tpu_custom_call" | custom-call | tf_op jit(solution)/shard_map/classify/pallas_call | solution.py:459
  32.6 0.8 %publish.1 = (f32[16,9216]{1,0:T(8,128)}, f32[1,16]{1,0:T(1,128)}, f32[1,8]{1,0:T(1,128)}) custom-call(f32[16,9216]{1,0:T(8,128)S(1)} %get-tuple-element.9.refs_0_, f32[1,16]{1,0:T(1,128)S(1)} %get-tuple-element.10.refs_1_, f32[1,8]{1,0:T(1,128)S(1)} %get-tuple-element.11.refs_2_), custom_call_target="tpu_custom_call" | custom-call | tf_op jit(solution)/shard_map/publish/pallas_call | solution.py:513

commit v3 on v2

--- a/solution.py
+++ b/solution.py
@@ -32,6 +32,8 @@
 SEG = LANE // LOW
 TILES = GROUPS * COLS
 WIDE = 2 * LANE
+CHUNK = 9
+CHUNKS = TILES // CHUNK
 BY_LANE = (((1,), (1,)), ((), ()))
 F32 = jnp.float32
 BF16 = jnp.bfloat16
@@ -91,11 +93,11 @@
 
 def kernel(
     n, m,
-    images_hbm, refs_hbm, prior_ref, ctf_ref, noise_ref, tau_ref, defocus_ref, offsets_ref, table_hbm,
+    images_hbm, refs_hbm, prior_hbm, ctf_hbm, noise_hbm, tau_hbm, defocus_hbm, offsets_hbm, table_hbm,
     fresh_ref, weight_ref, loglik_ref,
-    images_nat, refs_nat, table, own, every, spin, blend, unblend, turned, weighted_a, weighted_b, inserted,
-    acc, post, mixed, scales, stat, stats,
-    load_sem, left_sem, direct_sem, relay_left, relay_sem, stat_left, stat_sem, keep_sem, plane_sem,
+    images_nat, refs_nat, prior_ref, ctf_ref, noise_ref, tau_ref, defocus_ref, offsets_ref, table, own, every, spin, blend, unblend, turned, weighted, inserted, own_meta, metas, picks, phases, bright, quiet,
+    acc, post, mixed, inverses, stat, stats,
+    load_sem, left_sem, direct_sem, relay_left, relay_sem, stat_left, stat_sem, meta_left, meta_sem, keep_sem, plane_sem,
 ):
     local = images_nat.shape[0]
     owned = refs_nat.shape[0]
@@ -104,7 +106,6 @@
     width = stat.shape[1]
     height = ROT * owned
     step = MIX * owned
-    weighted = (weighted_a, weighted_b)
 
     row_id, column_id = lax.axis_index("img"), lax.axis_index("cls")
     partner = row_id + 1 - 2 * lax.rem(row_id, 2)
@@ -116,16 +117,16 @@
         for i in range(n) for c in range(m) if i or c
     ]
 
-    loads = [
-        pltpu.make_async_copy(images_hbm, images_nat, load_sem.at[0]),
-        pltpu.make_async_copy(refs_hbm, refs_nat, load_sem.at[1]),
-        pltpu.make_async_copy(table_hbm, table, load_sem.at[2]),
-    ]
-    for copy in loads:
-        copy.start()
     barrier = pltpu.get_barrier_semaphore()
     for peer in above + beside:
         pl.semaphore_signal(barrier, inc=1, device_id=peer, device_id_type=pl.DeviceIdType.MESH)
+    pairs = (
+        (images_hbm, images_nat), (defocus_hbm, defocus_ref), (offsets_hbm, offsets_ref), (refs_hbm, refs_nat),
+        (prior_hbm, prior_ref), (ctf_hbm, ctf_ref), (noise_hbm, noise_ref), (tau_hbm, tau_ref), (table_hbm, table),
+    )
+    loads = [pltpu.make_async_copy(src, dst, load_sem.at[k]) for k, (src, dst) in enumerate(pairs)]
+    for copy in loads:
+        copy.start()
 
     def send(src, dst, peer, left, landed):
         copy = pltpu.make_async_remote_copy(
@@ -145,14 +146,16 @@
         unblend[j, :LANE] = back
         unblend[j, LANE:] = back
 
-    meta = jnp.zeros((local, WIDE), F32)
-    lane = iota((local, WIDE), 1)
+    loads[1].wait()
+    loads[2].wait()
+    meta = jnp.zeros((local, LANE), F32)
+    lane = iota((local, LANE), 1)
     meta = jnp.where(lane == 0, column_of(defocus_ref[...].astype(F32), local), meta)
     for t in range(TRANS):
         for axis in range(2):
             value = column_of(offsets_ref[t, axis : axis + 1].astype(F32), local)
             meta = jnp.where(lane == 1 + t + axis * TRANS, value, meta)
-    own[0] = meta.astype(BF16)
+    own_meta[...] = meta.astype(BF16)
 
     def mix(nat, size, j):
         seg = iota((size, LANE), 1) // SEG
@@ -174,7 +177,7 @@
         for g in range(GROUPS):
             for p in range(2):
                 index = g * 2 + p
-                own[1 + g * COLS + j, :, p * LANE : (p + 1) * LANE] = moved[
+                own[g * COLS + j, :, p * LANE : (p + 1) * LANE] = moved[
                     index * local : (index + 1) * local
                 ]
 
@@ -182,24 +185,44 @@
     for peer in above:
         pl.semaphore_signal(plane_sem, inc=1, device_id=peer, device_id_type=pl.DeviceIdType.MESH)
 
-    def part_of(g):
-        return pl.ds(0, COLS + 1) if g == 0 else pl.ds(1 + g * COLS, COLS)
-
-    direct = [[None] * len(peers) for _ in range(GROUPS)]
-    relays = [[None] * (len(peers) + 1) for _ in range(GROUPS)]
-    for g in range(GROUPS):
-        piece = part_of(g)
-        for hop, peer in enumerate(peers):
-            direct[g][hop] = send(
-                own.at[piece], every.at[row_id, piece], {"img": peer}, left_sem.at[g, hop], direct_sem.at[g, hop]
-            )
-        relays[g][0] = send(
-            own.at[piece], every.at[row_id, piece], {"img": partner}, relay_left.at[g, 0], relay_sem.at[g, 0]
+    def remote(src, dst, peer, left, landed):
+        return pltpu.make_async_remote_copy(
+            src_ref=src, dst_ref=dst, send_sem=left, recv_sem=landed,
+            device_id=peer, device_id_type=pl.DeviceIdType.MESH,
         )
-    keep = pltpu.make_async_copy(own, every.at[row_id], keep_sem.at[0])
-    keep.start()
-
-    loads[1].wait()
+
+    def outward(c, hop):
+        piece = pl.ds(c * CHUNK, CHUNK)
+        return remote(
+            own.at[piece], every.at[row_id, piece], {"img": peers[hop]}, left_sem.at[c, hop], direct_sem.at[c, hop]
+        )
+
+    def relay(c, hop):
+        piece = pl.ds(c * CHUNK, CHUNK)
+        if hop == 0:
+            src, dst = own.at[piece], every.at[row_id, piece]
+        else:
+            src = dst = every.at[lax.rem(row_id + n - 2 * hop, n), piece]
+        return remote(src, dst, {"img": partner}, relay_left.at[c, hop], relay_sem.at[c, hop])
+
+    def titles(hop):
+        return remote(own_meta, metas.at[row_id], beside[hop], meta_left.at[hop], meta_sem.at[hop])
+
+    hops = len(peers)
+    for hop in range(n - 1):
+        titles(hop).start()
+    for c in range(CHUNKS):
+        for hop in range(hops):
+            outward(c, hop).start()
+        relay(c, 0).start()
+    keeps = [
+        pltpu.make_async_copy(own, every.at[row_id], keep_sem.at[0]),
+        pltpu.make_async_copy(own_meta, metas.at[row_id], keep_sem.at[1]),
+    ]
+    for copy in keeps:
+        copy.start()
+    acc[...] = jnp.zeros(acc.shape, F32)
+    loads[3].wait()
     for j in range(COLS):
         spin[j] = mix(refs_nat, owned, j)
     lane = iota((2 * GROUPS * owned, LANE), 1)
@@ -235,39 +258,36 @@
     def widen(value):
         return jnp.dot(value, spread, precision=HIGH, preferred_element_type=F32)
 
+    for copy in loads[4:8]:
+        copy.wait()
     ctf_wide = widen(ctf_ref[...])
     noise_wide = widen(jnp.broadcast_to(noise_ref[...], (8, CYCLES)))[:1]
     tau_wide = widen(jnp.broadcast_to(1.0 / tau_ref[...], (8, CYCLES)))[:1]
     prior = column_of(prior_ref[...].astype(F32), owned)
 
-    def arrive(g):
-        piece = part_of(g)
-        for hop, copy in enumerate(direct[g]):
-            copy.wait_recv()
-            origin = lax.rem(row_id + n - 2 * (hop + 1), n)
-            slot = every.at[origin, piece]
-            relays[g][hop + 1] = send(
-                slot, slot, {"img": partner}, relay_left.at[g, hop + 1], relay_sem.at[g, hop + 1]
-            )
-
-    def settle(g):
-        for copy in relays[g]:
-            copy.wait_recv()
+    def arrive(c):
+        for hop in range(hops):
+            outward(c, hop).wait_recv()
+            relay(c, hop + 1).start()
+
+    def settle(c):
+        for hop in range(hops + 1):
+            relay(c, hop).wait_recv()
 
     def setup():
-        meta = every[:, 0].astype(F32).reshape(count, WIDE)
+        meta = metas[...].astype(F32).reshape(count, LANE)
         group = iota((count, NDEF), 1).astype(F32)
         chosen = onehot(group == meta[:, :1])
         contrast = jnp.dot(chosen, ctf_wide, precision=HIGH, preferred_element_type=F32)
         square = contrast * contrast
         spot = iota((count, TABLE_ROWS), 1).astype(F32)
         lane = iota((count, LANE), 1)
-        picks, terms = [], []
+        terms = []
         for t in range(TRANS):
             dx = meta[:, 1 + t : 2 + t]
             dy = meta[:, 1 + TRANS + t : 2 + TRANS + t]
             index = (dx + REACH) * SIDE + (dy + REACH)
-            picks.append(onehot((spot == index) | (spot == index + COMBOS)).astype(BF16))
+            picks[t * count : (t + 1) * count] = onehot((spot == index) | (spot == index + COMBOS)).astype(BF16)
             value = -(dx * dx + dy * dy) / (2.0 * offset_sigma * offset_sigma)
             terms.append(jnp.where(lane == 0, value, 0.0))
         coef = square / (2.0 * noise_wide)
@@ -277,50 +297,62 @@
             jnp.ones((owned, LANE), F32), jnp.concatenate(terms, axis=0), BY_LANE,
             precision=HIGH, preferred_element_type=F32,
         )
-        return picks, contrast, square, contrast / noise_wide, base
-
-    def build(g, picks, contrast, scaled, slot):
-        bright = contrast[:, g * LANE : (g + 1) * LANE]
-        scale = scaled[:, g * LANE : (g + 1) * LANE]
-        for j in range(COLS):
-            tile = g * COLS + j
-            picture = every[:, 1 + tile].astype(F32).reshape(count, WIDE)
-            real, imag = picture[:, :LANE], picture[:, LANE:]
-            for t in range(TRANS):
-                phase = jnp.dot(picks[t], table[tile], preferred_element_type=F32)
-                cosine, sine = phase[:, :LANE], phase[:, LANE:]
-                moved_real = real * cosine - imag * sine
-                moved_imag = real * sine + imag * cosine
-                span = slice(t * count, (t + 1) * count)
-                inserted[tile, span, :LANE] = (moved_real * bright).astype(BF16)
-                inserted[tile, span, LANE:] = (moved_imag * bright).astype(BF16)
-                slot[span, j * WIDE : j * WIDE + LANE] = (moved_real * scale).astype(BF16)
-                slot[span, j * WIDE + LANE : (j + 1) * WIDE] = (moved_imag * scale).astype(BF16)
-
-    def score(g, slot):
-        left = jnp.concatenate(
-            [turned[g, (COLS - j) * step : (COLS - j) * step + height] for j in range(COLS)], axis=1
+        calm = 1.0 / noise_wide
+        for g in range(GROUPS):
+            bright[g] = contrast[:, g * LANE : (g + 1) * LANE]
+            quiet[g : g + 1] = calm[:, g * LANE : (g + 1) * LANE]
+        return square, base
+
+    def prepare(begin, end):
+        @pl.loop(begin // 6, end // 6)
+        def _(block):
+            for place in range(6):
+                tile = block * 6 + place
+                phases[tile] = jnp.dot(picks[...], table[tile], preferred_element_type=F32)
+
+    def shifted(tile):
+        light = bright[lax.div(tile, COLS)]
+        picture = every[:, tile].astype(F32).reshape(count, WIDE)
+        real, imag = picture[:, :LANE] * light, picture[:, LANE:] * light
+        for t in range(TRANS):
+            span = slice(t * count, (t + 1) * count)
+            cosine, sine = phases[tile, span, :LANE], phases[tile, span, LANE:]
+            yield span, real * cosine - imag * sine, real * sine + imag * cosine
+
+    def build(tile, place, slot):
+        calm = quiet[pl.ds(lax.div(tile, COLS), 1)]
+        for span, real, imag in shifted(tile):
+            inserted[tile, span, :LANE] = real.astype(BF16)
+            inserted[tile, span, LANE:] = imag.astype(BF16)
+            slot[span, place * WIDE : place * WIDE + LANE] = (real * calm).astype(BF16)
+            slot[span, place * WIDE + LANE : (place + 1) * WIDE] = (imag * calm).astype(BF16)
+
+    loads[8].wait()
+    for copy in keeps:
+        copy.wait()
+    for hop in range(n - 1):
+        titles(hop).wait_recv()
+    square, base = setup()
+    prepare(0, TILES // 2)
+    arrive(0)
+    prepare(TILES // 2, TILES)
+
+    @pl.loop(0, CHUNKS)
+    def _(c):
+        @pl.when(c + 1 < CHUNKS)
+        def _():
+            arrive(c + 1)
+
+        settle(c)
+        lefts = []
+        for place in range(CHUNK):
+            tile = c * CHUNK + place
+            build(tile, place, weighted)
+            g, j = lax.div(tile, COLS), lax.rem(tile, COLS)
+            lefts.append(turned[g, pl.ds(pl.multiple_of((COLS - j) * step, step), height)])
+        acc[...] += lax.dot_general(
+            jnp.concatenate(lefts, axis=1), weighted[...], BY_LANE, preferred_element_type=F32
         )
-        value = lax.dot_general(left, slot[...], BY_LANE, preferred_element_type=F32)
-        if g == 0:
-            acc[...] = value
-        else:
-            acc[...] += value
-
-    loads[2].wait()
-    keep.wait()
-    arrive(0)
-    settle(0)
-    picks, contrast, square, scaled, base = setup()
-    for g in range(GROUPS):
-        if g + 1 < GROUPS:
-            arrive(g + 1)
-        if g:
-            settle(g)
-        build(g, picks, contrast, scaled, weighted[g % 2])
-        if g:
-            score(g - 1, weighted[(g - 1) % 2])
-    score(GROUPS - 1, weighted[(GROUPS - 1) % 2])
 
     def over_shifts(value, combine):
         total = value
@@ -386,16 +418,17 @@
     lane = iota((owned, LANE), 1)
     seg = iota((owned, LANE), 1) // SEG
     for g in range(GROUPS):
-        scales[g] = inverse[:, g * LANE : (g + 1) * LANE]
-
-    @pl.loop(0, GROUPS)
-    def _(g):
+        inverses[g] = inverse[:, g * LANE : (g + 1) * LANE]
+
+    def insert(g):
         left = jnp.concatenate(
             [post[(COLS - s) * step : (COLS - s) * step + height] for s in range(COLS)], axis=1
         )
         right = jnp.concatenate([inserted[g * COLS + s] for s in range(COLS)], axis=0)
-        mixed[...] = jnp.dot(left, right, preferred_element_type=F32)
-        scale = scales[g]
+        return jnp.dot(left, right, preferred_element_type=F32)
+
+    def finish(g):
+        scale = inverses[g]
         spread_out = [[], []]
         for j in range(COLS):
             halves = []
@@ -418,13 +451,32 @@
                 spread_out[p].append(value[p * owned : (p + 1) * owned])
         for p in range(2):
             for k in range(COLS):
-                start = pl.multiple_of(g * SPAN + (p * CYCLES * ANG + k * LANE), LANE)
+                start = g * SPAN + (p * CYCLES * ANG + k * LANE)
+                if not isinstance(g, int):
+                    start = pl.multiple_of(start, LANE)
                 fresh_ref[:, pl.ds(start, LANE)] = pick_segments(
                     [spread_out[p][(LOW * k + s) % COLS] for s in range(LOW)], seg
                 )
 
-    for copy in sum(direct, []) + sum(relays, []) + shared:
+    mixed[...] = insert(0)
+
+    @pl.loop(1, GROUPS)
+    def _(g):
+        value = insert(g)
+        finish(g - 1)
+        mixed[...] = value
+
+    finish(GROUPS - 1)
+
+    for copy in shared + [titles(hop) for hop in range(n - 1)]:
         copy.wait_send()
+
+    @pl.loop(0, CHUNKS)
+    def _(c):
+        for hop in range(hops):
+            outward(c, hop).wait_send()
+        for hop in range(hops + 1):
+            relay(c, hop).wait_send()
 
 
 def publish(*refs):
@@ -463,35 +515,48 @@
             pltpu.VMEM((1, owned), F32),
             pltpu.VMEM((1, local), F32),
         ),
-        in_specs=[hbm, hbm] + [vmem] * 6 + [hbm],
+        in_specs=[hbm] * 9,
         out_specs=(vmem,) * 3,
         scratch_shapes=[
             pltpu.VMEM((local, 2 * CYCLES * ANG), BF16),
             pltpu.VMEM((owned, 2 * CYCLES * ANG), BF16),
+            pltpu.VMEM((1, owned), prior.dtype),
+            pltpu.VMEM(ctf_table.shape, F32),
+            pltpu.VMEM((1, CYCLES), F32),
+            pltpu.VMEM((1, CYCLES), F32),
+            pltpu.VMEM((1, local), jnp.int32),
+            pltpu.VMEM((TRANS, 2, local), jnp.int32),
             pltpu.VMEM((TILES, TABLE_ROWS, WIDE), BF16),
-            pltpu.VMEM((1 + TILES, local, WIDE), BF16),
-            pltpu.VMEM((n, 1 + TILES, local, WIDE), BF16),
+            pltpu.VMEM((TILES, local, WIDE), BF16),
+            pltpu.VMEM((n, TILES, local, WIDE), BF16),
             pltpu.VMEM((COLS, 2 * GROUPS * owned, LANE), F32),
             pltpu.VMEM((LOW, LANE, LANE), BF16),
             pltpu.VMEM((LOW, WIDE, LANE), BF16),
             pltpu.VMEM((GROUPS, 2 * height, WIDE), BF16),
-            pltpu.VMEM((rows, COLS * WIDE), BF16),
-            pltpu.VMEM((rows, COLS * WIDE), BF16),
+            pltpu.VMEM((rows, CHUNK * WIDE), BF16),
             pltpu.VMEM((TILES, rows, WIDE), BF16),
+            pltpu.VMEM((local, LANE), BF16),
+            pltpu.VMEM((n, local, LANE), BF16),
+            pltpu.VMEM((rows, TABLE_ROWS), BF16),
+            pltpu.VMEM((TILES, rows, WIDE), F32),
+            pltpu.VMEM((GROUPS, count, LANE), F32),
+            pltpu.VMEM((GROUPS, LANE), F32),
             pltpu.VMEM((height, rows), F32),
             pltpu.VMEM((2 * height, rows), BF16),
             pltpu.VMEM((height, WIDE), F32),
             pltpu.VMEM((GROUPS, owned, LANE), F32),
             pltpu.VMEM((2, width), F32),
             pltpu.VMEM((n, m, 2, width), F32),
-            dma((3,)),
-            dma((GROUPS, hops)),
-            dma((GROUPS, hops)),
-            dma((GROUPS, hops + 1)),
-            dma((GROUPS, hops + 1)),
+            dma((9,)),
+            dma((CHUNKS, hops)),
+            dma((CHUNKS, hops)),
+            dma((CHUNKS, hops + 1)),
+            dma((CHUNKS, hops + 1)),
             dma((n * m - 1,)),
             dma((n * m - 1,)),
-            dma((1,)),
+            dma((n - 1,)),
+            dma((n - 1,)),
+            dma((2,)),
             pltpu.SemaphoreType.REGULAR,
         ],
         compiler_params=pltpu.CompilerParams(

time: 33.7 us -> 29.5 us (0.88)
  Pallas kernels: 32.8 us -> 28.7 us
    pallas_call x1, Pallas kernels: 32 us -> 27.9 us  [per_device(): pl.pallas_call(lambda *refs: kernel(n, m, *refs), out_shape=(pltpu.VMEM((...]
where the time goes in v3:
time: 29.5 us; the launch traced here: 29.4 us
  Pallas kernels  28.7 us (97%)
  between operations  0.64 us (2%)
    pallas_call x1, Pallas kernels, per_device(): pl.pallas_call(lambda *refs: kernel(n, m, *refs), out_shape=(pltpu.VMEM((...  27.9 us
    pallas_call x1, Pallas kernels, per_device(): pl.pallas_call(publish, out_shape=tuple((jax.ShapeDtypeStruct(shape, F32)...  0.85 us

profile of v3, /device:TPU:0, one launch (start us, length us, event | category | flops | bytes accessed | tf_op | source)
XLA Modules:
  0.0 29.4 jit_solution(13758456873506001128)
XLA Ops:
  0.6 27.9 %classify.1 = (f32[16,9216]{1,0:T(8,128)S(1)}, f32[1,16]{1,0:T(1,128)S(1)}, f32[1,8]{1,0:T(1,128)S(1)}) custom-call(bf16[8,9216]{1,0:T(8,128)(2,1)} %refs_0_.1, bf16[16,9216]{1,0:T(8,128)(2,1)} %refs_1_.1, bf16[1,16]{1,0:T(2,128)(2,1)} %bitcast.8, f32[16,32]{1,0:T(8,128)} %refs_3_.1, f32[1,32]{1,0:T(1,128)} %bitcast.9, f32[1,32]{1,0:T(1,128)} %bitcast.10, ...), custom_call_target="tpu_custom_call" | custom-call | tf_op jit(solution)/shard_map/classify/pallas_call | solution.py:511
  28.5 0.8 %publish.1 = (f32[16,9216]{1,0:T(8,128)}, f32[1,16]{1,0:T(1,128)}, f32[1,8]{1,0:T(1,128)}) custom-call(f32[16,9216]{1,0:T(8,128)S(1)} %get-tuple-element.9.refs_0_, f32[1,16]{1,0:T(1,128)S(1)} %get-tuple-element.10.refs_1_, f32[1,8]{1,0:T(1,128)S(1)} %get-tuple-element.11.refs_2_), custom_call_target="tpu_custom_call" | custom-call | tf_op jit(solution)/shard_map/publish/pallas_call | solution.py:578
